TPU v7x, 256 devices: a 2x2x32 block of a 4x8x32 slice. The times are simulated.
256 devices in a mesh: groups: 4 (over x, y), seq: 64 (over z, core).
Axes of the slice: x: 2, y: 2, z: 32, core: 2. Of those that a mesh axis runs over, the one named last changes fastest.
The devices are a block of a 4x8x32 slice.
Arguments:
- queries: bfloat16 [65536, 4096], P(('groups', 'seq')), parts along dimension 0, may hold values from -6 to 6
- keys: bfloat16 [65536, 2048], P(('groups', 'seq')), parts along dimension 0, may hold values from -6 to 6
- values: bfloat16 [65536, 2048], P(('groups', 'seq')), parts along dimension 0, may hold values from -6 to 6
- doc_blocks: int32 [32], P('groups'), parts along dimension 0, may hold values from 1 to 32, 128 in all
Outputs:
- attended: bfloat16 [65536, 4096], P(('groups', 'seq')), parts along dimension 0
There are 4 independent parts, one for each index of `groups`. A program takes and returns all parts, laid end to end along the dimension named above; each array names one. Nothing has to cross between parts.
Inputs may be any that keep to these rules, and one draw needn't show every extreme that they name: `doc_blocks`: the lengths add up to 128; the longest document has exactly 32 units.
All inputs are finite; a program needn't handle non-finite values.
Results may differ from a plain program's by a relative error of at most 0.004.
Values may be sent and summed in bfloat16 or wider, within the bound.
A program may use at most 64 MiB of HBM per device.

v0:
```python
import functools

import jax
import jax.numpy as jnp
from jax import lax
from jax.experimental import pallas as pl
from jax.experimental.pallas import tpu as pltpu
from jax.sharding import PartitionSpec as P

DH = 128
BLK = 128
MAX_UNITS = 32
MESH = pl.DeviceIdType.MESH
LOG2E = 1.4426950408889634
SCALE = 144.0 ** (-0.5) * LOG2E
HIDDEN = -1e30
FLOOR = -1e29


def kernel(
    chips, reach, tail, docs_ref, q_hbm, k_hbm, v_hbm, o_hbm,
    q_all, own, got, run_max, run_sum, acc, result,
    load_sem, pair_send, pair_recv, ring_send, ring_recv, out_sem, back_send, back_recv,
):
    rows = q_hbm.shape[0]
    both = 2 * rows
    keys_here = own.shape[0]
    heads_here = q_all.shape[0]
    ratio = heads_here // keys_here
    blocks = both // BLK
    me = lax.axis_index("seq")
    core = lax.rem(me, 2)
    chip = lax.div(me, 2)
    partner = me + 1 - 2 * core
    right = lax.rem(chip + 1, chips) * 2 + core
    left = lax.rem(chip + chips - 1, chips) * 2 + core

    barrier = pltpu.get_barrier_semaphore()
    for source in (left, partner):
        pl.semaphore_signal(barrier, inc=1, device_id={"seq": source}, device_id_type=MESH)
    pl.semaphore_wait(barrier, 2)

    mine = pl.ds(pl.multiple_of(core * rows, rows), rows)
    theirs = pl.ds(pl.multiple_of((1 - core) * rows, rows), rows)

    def columns(head):
        return pl.ds(pl.multiple_of(head * DH, DH), DH)

    def pieces(index, side, place):
        first = side * keys_here + index
        listed = [
            (k_hbm.at[:, columns(first)], own.at[index, 0, place], index),
            (v_hbm.at[:, columns(first)], own.at[index, 1, place], keys_here + index),
        ]
        for j in range(ratio):
            head = index * ratio + j
            listed.append(
                (
                    q_hbm.at[:, columns(side * heads_here + head)],
                    q_all.at[head, place],
                    2 * keys_here + head,
                )
            )
        return listed

    def local_copy(entry):
        return pltpu.make_async_copy(entry[0], entry[1], load_sem.at[entry[2]])

    def pair_copy(entry):
        return pltpu.make_async_remote_copy(
            src_ref=entry[0], dst_ref=entry[1],
            send_sem=pair_send.at[entry[2]], recv_sem=pair_recv.at[entry[2]],
            device_id={"seq": partner}, device_id_type=MESH,
        )

    def start_kv(g, carry):
        for entry in pieces(g, 1 - core, mine)[:2]:
            pair_copy(entry).start()
        for entry in pieces(g, core, mine)[:2]:
            local_copy(entry).start()
        return carry

    def start_q(g, carry):
        for entry in pieces(g, 1 - core, mine)[2:]:
            pair_copy(entry).start()
        for entry in pieces(g, core, mine)[2:]:
            local_copy(entry).start()
        return carry

    lax.fori_loop(0, keys_here, start_kv, 0)
    lax.fori_loop(0, keys_here, start_q, 0)

    def hop(source, step, g, partial):
        rows_sent = pl.ds(both - tail, tail) if partial else pl.ds(0, both)
        return pltpu.make_async_remote_copy(
            src_ref=source.at[:, rows_sent], dst_ref=got.at[step, g, :, rows_sent],
            send_sem=ring_send.at[step, g], recv_sem=ring_recv.at[step, g],
            device_id={"seq": right}, device_id_type=MESH,
        )

    def first_send(g, carry):
        for entry in pieces(g, core, mine)[:2]:
            local_copy(entry).wait()
        for entry in pieces(g, 1 - core, theirs)[:2]:
            pair_copy(entry).wait_recv()
        hop(own.at[g], 0, g, reach == 1).start()
        return carry

    lax.fori_loop(0, keys_here, first_send, 0)

    def wait_q(g, carry):
        for entry in pieces(g, core, mine)[2:]:
            local_copy(entry).wait()
        for entry in pieces(g, 1 - core, theirs)[2:]:
            pair_copy(entry).wait_recv()
        return carry

    lax.fori_loop(0, keys_here, wait_q, 0)

    starts = []
    for b in range(blocks):
        block = chip * blocks + b
        end = jnp.int32(0)
        start = jnp.int32(0)
        for d in range(docs_ref.shape[0]):
            end = end + docs_ref[d]
            start = jnp.where(block >= end, end, start)
        starts.append(start * BLK)

    def flash(g, source, first_key, skip, causal):
        count = both - skip
        k = source[0, pl.ds(skip, count), :]
        v = source[1, pl.ds(skip, count), :]
        lane = lax.broadcasted_iota(jnp.int32, (ratio * BLK, count), 1) + (first_key + skip)
        for b in range(blocks):
            span = pl.ds(b * BLK, BLK)
            q = q_all[pl.ds(g * ratio, ratio), span, :].reshape(ratio * BLK, DH)
            s = lax.dot_general(q, k, (((1,), (1,)), ((), ())), preferred_element_type=jnp.float32)
            visible = lane >= starts[b]
            if causal:
                row = lax.broadcasted_iota(jnp.int32, (ratio, BLK, count), 1).reshape(ratio * BLK, count)
                visible = visible & (lane <= row + (chip * both + b * BLK))
            s = jnp.where(visible, s * SCALE, HIDDEN)
            top = jnp.max(s, axis=1, keepdims=True)
            if causal:
                new_max = jnp.maximum(jnp.full((ratio * BLK, DH), FLOOR, jnp.float32), top)
            else:
                old_max = run_max[g, b]
                new_max = jnp.maximum(old_max, top)
            p = jnp.exp2(s - new_max[:, :1])
            total = jnp.sum(p, axis=1, keepdims=True)
            fresh = jnp.dot(p.astype(jnp.bfloat16), v, preferred_element_type=jnp.float32)
            if causal:
                run_sum[g, b] = jnp.broadcast_to(total, (ratio * BLK, DH))
                acc[g, b] = fresh
            else:
                shrink = jnp.exp2(old_max - new_max)
                run_sum[g, b] = run_sum[g, b] * shrink + total
                acc[g, b] = acc[g, b] * shrink + fresh
            run_max[g, b] = new_max

    def own_block(g, carry):
        flash(g, own.at[g], chip * both, 0, True)
        return carry

    lax.fori_loop(0, keys_here, own_block, 0)

    def out_copy(head):
        return pltpu.make_async_copy(
            result.at[head, mine], o_hbm.at[:, columns(core * heads_here + head)], out_sem.at[head]
        )

    def back_copy(head, side):
        return pltpu.make_async_remote_copy(
            src_ref=result.at[head, theirs],
            dst_ref=o_hbm.at[:, columns(side * heads_here + head)],
            send_sem=back_send.at[head], recv_sem=back_recv.at[head],
            device_id={"seq": partner}, device_id_type=MESH,
        )

    def finish(g):
        for b in range(blocks):
            value = (acc[g, b] / run_sum[g, b]).astype(jnp.bfloat16).reshape(ratio, BLK, DH)
            result[pl.ds(g * ratio, ratio), pl.ds(b * BLK, BLK), :] = value

    def send_back(g):
        for j in range(ratio):
            back_copy(g * ratio + j, core).start()
            out_copy(g * ratio + j).start()

    def middle(index, carry):
        step = index // keys_here
        g = index % keys_here
        source = got.at[step, g]
        hop(source, step, g, False).wait_recv()

        @pl.when(step < reach - 2)
        def _():
            hop(source, step + 1, g, False).start()

        @pl.when(step == reach - 2)
        def _():
            hop(source, reach - 1, g, True).start()

        flash(g, source, (chip - 1 - step) * both, 0, False)
        return carry

    lax.fori_loop(0, (reach - 1) * keys_here, middle, 0)

    def last(g, carry):
        source = got.at[reach - 1, g]
        hop(source, reach - 1, g, True).wait_recv()
        flash(g, source, (chip - reach) * both, both - tail, False)
        finish(g)

        @pl.when(g > 0)
        def _():
            send_back(g - 1)

        return carry

    lax.fori_loop(0, keys_here, last, 0)
    send_back(keys_here - 1)

    def drain(g, carry):
        for entry in pieces(g, 1 - core, mine):
            pair_copy(entry).wait_send()
        for step in range(reach):
            hop(own.at[g], step, g, step == reach - 1).wait_send()
        for j in range(ratio):
            head = g * ratio + j
            out_copy(head).wait()
            back_copy(head, core).wait_send()
            back_copy(head, 1 - core).wait_recv()
        return carry

    lax.fori_loop(0, keys_here, drain, 0)


def on_device(queries, keys, values, doc_blocks):
    rows = queries.shape[0]
    both = 2 * rows
    chips = lax.axis_size("seq") // 2
    heads_here = queries.shape[1] // DH // 2
    keys_here = keys.shape[1] // DH // 2
    ratio = heads_here // keys_here
    blocks = both // BLK
    back = (MAX_UNITS - 1) * BLK
    reach = -(-back // both)
    tail = back - (reach - 1) * both
    state = (keys_here, blocks, ratio * BLK, DH)
    pieces = 2 * keys_here + heads_here
    anywhere = pl.BlockSpec(memory_space=pl.ANY)
    return pl.pallas_call(
        functools.partial(kernel, chips, reach, tail),
        out_shape=jax.ShapeDtypeStruct(queries.shape, queries.dtype),
        in_specs=[pl.BlockSpec(memory_space=pltpu.SMEM)] + [anywhere] * 3,
        out_specs=anywhere,
        scratch_shapes=[
            pltpu.VMEM((heads_here, both, DH), jnp.bfloat16),
            pltpu.VMEM((keys_here, 2, both, DH), jnp.bfloat16),
            pltpu.VMEM((reach, keys_here, 2, both, DH), jnp.bfloat16),
            pltpu.VMEM(state, jnp.float32),
            pltpu.VMEM(state, jnp.float32),
            pltpu.VMEM(state, jnp.float32),
            pltpu.VMEM((heads_here, both, DH), jnp.bfloat16),
            pltpu.SemaphoreType.DMA((pieces,)),
            pltpu.SemaphoreType.DMA((pieces,)),
            pltpu.SemaphoreType.DMA((pieces,)),
            pltpu.SemaphoreType.DMA((reach, keys_here)),
            pltpu.SemaphoreType.DMA((reach, keys_here)),
            pltpu.SemaphoreType.DMA((heads_here,)),
            pltpu.SemaphoreType.DMA((heads_here,)),
            pltpu.SemaphoreType.DMA((heads_here,)),
        ],
        compiler_params=pltpu.CompilerParams(
            collective_id=0, has_side_effects=True, vmem_limit_bytes=60 * 1024 * 1024
        ),
        name="forward_attention",
    )(doc_blocks, queries, keys, values)


def solution(mesh):
    token = P(("groups", "seq"), None)
    return jax.shard_map(
        on_device, mesh=mesh, in_specs=(token, token, token, P("groups")),
        out_specs=token, check_vma=False,
    )
```

profile of v0, /device:TPU:37, one launch (start us, length us, event | category | flops | bytes accessed | tf_op | source)
XLA Modules:
  0.0 384.5 jit_solution(6427564132617776572)
XLA Ops:
  0.0 381.4 %forward_attention.1 = bf16[256,4096]{1,0:T(8,128)(2,1)} custom-call(s32[8]{0:T(128)} %docs_ref.1, bf16[256,4096]{1,0:T(8,128)(2,1)} %q_hbm.1, bf16[256,2048]{1,0:T(8,128)(2,1)} %k_hbm.1, bf16[256,2048]{1,0:T(8,128)(2,1)} %v_hbm.1), custom_call_target="tpu_custom_call" | custom-call | tf_op jit(solution)/shard_map/forward_attention/pallas_call | solution.py:254
  381.4 3.1 copy.6
where the time goes:
time: 385 us; the launch traced here: 384 us
  Pallas kernels  381 us (99%)
    pallas_call x1, Pallas kernels, on_device(): pl.pallas_call(functools.partial(kernel, chips, reach, tail), out_shape=j...  381 us

commit v1 on v0

v1 whole, which is shorter than its diff:
```python
import functools

import jax
import jax.numpy as jnp
from jax import lax
from jax.experimental import pallas as pl
from jax.experimental.pallas import tpu as pltpu
from jax.sharding import PartitionSpec as P

DH = 128
BLK = 128
MAX_UNITS = 32
MESH = pl.DeviceIdType.MESH
LOG2E = 1.4426950408889634
SCALE = 144.0 ** (-0.5) * LOG2E
HIDDEN = -1e30
FLOOR = -1e29
FAR = 1 << 30


def kernel(
    chips, span, docs_ref, q_hbm, k_hbm, v_hbm, o_hbm,
    q_all, own, turned, got, sent, got_stat, sent_stat, q_got,
    run_max, run_sum, acc, part, part_stat, result,
    load_sem, pair_send, pair_recv, ring_send, ring_recv, stat_send, stat_recv,
    q_send, q_recv, out_sem, back_send, back_recv,
):
    rows = q_hbm.shape[0]
    both = 2 * rows
    keys_here = own.shape[0]
    heads_here = q_all.shape[0]
    ratio = heads_here // keys_here
    blocks = both // BLK
    fixed = keys_here // 2
    me = lax.axis_index("seq")
    core = lax.rem(me, 2)
    chip = lax.div(me, 2)
    partner = me + 1 - 2 * core
    right = lax.rem(chip + 1, chips) * 2 + core
    left = lax.rem(chip + chips - 1, chips) * 2 + core

    barrier = pltpu.get_barrier_semaphore()
    for source in (left, right, partner):
        pl.semaphore_signal(barrier, inc=1, device_id={"seq": source}, device_id_type=MESH)
    pl.semaphore_wait(barrier, 3)

    mine = pl.ds(pl.multiple_of(core * rows, rows), rows)
    theirs = pl.ds(pl.multiple_of((1 - core) * rows, rows), rows)

    def columns(head):
        return pl.ds(pl.multiple_of(head * DH, DH), DH)

    def block_rows(b):
        return pl.ds(pl.multiple_of(b * BLK, BLK), BLK)

    def kv_pieces(index, side, place):
        first = side * keys_here + index
        return [
            (k_hbm.at[:, columns(first)], own.at[index, 0, place], index),
            (v_hbm.at[:, columns(first)], own.at[index, 1, place], keys_here + index),
        ]

    def q_pieces(index, side, place):
        listed = []
        for j in range(ratio):
            head = index * ratio + j
            listed.append(
                (
                    q_hbm.at[:, columns(side * heads_here + head)],
                    q_all.at[head, place],
                    2 * keys_here + head,
                )
            )
        return listed

    def local_copy(entry):
        return pltpu.make_async_copy(entry[0], entry[1], load_sem.at[entry[2]])

    def pair_copy(entry):
        return pltpu.make_async_remote_copy(
            src_ref=entry[0], dst_ref=entry[1],
            send_sem=pair_send.at[entry[2]], recv_sem=pair_recv.at[entry[2]],
            device_id={"seq": partner}, device_id_type=MESH,
        )

    def load(kind, index):
        for entry in kind(index, 1 - core, mine):
            pair_copy(entry).start()
        for entry in kind(index, core, mine):
            local_copy(entry).start()

    def arrive(kind, index):
        for entry in kind(index, core, mine):
            local_copy(entry).wait()
        for entry in kind(index, 1 - core, theirs):
            pair_copy(entry).wait_recv()

    def hop(source, phase, slot, b):
        return pltpu.make_async_remote_copy(
            src_ref=source, dst_ref=got.at[phase, slot, b],
            send_sem=ring_send.at[phase % 2, slot, b], recv_sem=ring_recv.at[phase, slot, b],
            device_id={"seq": right}, device_id_type=MESH,
        )

    def stat_hop(phase, slot, b):
        return pltpu.make_async_remote_copy(
            src_ref=sent_stat.at[phase % 2, slot, b], dst_ref=got_stat.at[phase, slot, b],
            send_sem=stat_send.at[phase % 2, slot, b], recv_sem=stat_recv.at[phase, slot, b],
            device_id={"seq": right}, device_id_type=MESH,
        )

    def q_hop(source, phase, slot, b):
        return pltpu.make_async_remote_copy(
            src_ref=source, dst_ref=q_got.at[phase, slot, b],
            send_sem=q_send.at[phase, slot, b], recv_sem=q_recv.at[phase, slot, b],
            device_id={"seq": left}, device_id_type=MESH,
        )

    def own_q(phase, b):
        return q_all.at[pl.ds((fixed + phase) * ratio, ratio), block_rows(b)]

    load(kv_pieces, 0)
    load(q_pieces, fixed)

    def start_rest(g, carry):
        load(kv_pieces, fixed + g)

        @pl.when(g > 0)
        def _():
            load(q_pieces, fixed + g)
            load(kv_pieces, g)

        load(q_pieces, g)
        return carry

    lax.fori_loop(0, fixed, start_rest, 0)

    arrive(kv_pieces, 0)
    for b in range(blocks):
        hop(own.at[0, :, block_rows(b)], 0, 0, b).start()
    arrive(q_pieces, fixed)
    for b in range(blocks):
        q_hop(own_q(0, b), 0, 0, b).start()

    def wait_rest(g, carry):
        arrive(kv_pieces, fixed + g)

        @pl.when(g > 0)
        def _():
            arrive(q_pieces, fixed + g)
            arrive(kv_pieces, g)

        arrive(q_pieces, g)
        turned[g] = own[fixed + g, 1].astype(jnp.float32).T.astype(jnp.bfloat16)
        return carry

    lax.fori_loop(0, fixed, wait_rest, 0)

    def unit(index):
        total = jnp.int32(0)
        start = jnp.int32(0)
        end = jnp.int32(FAR)
        for d in range(docs_ref.shape[0]):
            total = total + docs_ref[d]
            start = jnp.where(index >= total, total, start)
            end = jnp.minimum(end, jnp.where(index >= total, FAR, total))
        return start, end

    first = chip * blocks
    here_start, here_end = unit(first + blocks - 1)
    keys_from = jnp.where(here_end > first + blocks, here_start, FAR)
    _, before_end = unit(first - 1)
    sums_to = jnp.where((before_end > first) & (chip > 0), before_end, 0)

    def flash(g, b, k, v, first_key, causal):
        start = unit(first + b)[0] * BLK
        lane = lax.broadcasted_iota(jnp.int32, (ratio * BLK, both), 1) + first_key
        q = q_all[pl.ds(g * ratio, ratio), block_rows(b), :].reshape(ratio * BLK, DH)
        s = lax.dot_general(q, k, (((1,), (1,)), ((), ())), preferred_element_type=jnp.float32)
        visible = lane >= start
        if causal:
            row = lax.broadcasted_iota(jnp.int32, (ratio, BLK, both), 1).reshape(ratio * BLK, both)
            visible = visible & (lane <= row + (first_key + b * BLK))
        s = jnp.where(visible, s * SCALE, HIDDEN)
        top = jnp.max(s, axis=1, keepdims=True)
        if causal:
            new_max = jnp.maximum(jnp.full((ratio * BLK, DH), FLOOR, jnp.float32), top)
        else:
            old_max = run_max[g, b]
            new_max = jnp.maximum(old_max, top)
        p = jnp.exp2(s - new_max[:, :1])
        total = jnp.sum(p, axis=1, keepdims=True)
        fresh = jnp.dot(p.astype(jnp.bfloat16), v, preferred_element_type=jnp.float32)
        if causal:
            run_sum[g, b] = jnp.broadcast_to(total, (ratio * BLK, DH))
            acc[g, b] = fresh
        else:
            shrink = jnp.exp2(old_max - new_max)
            run_sum[g, b] = run_sum[g, b] * shrink + total
            acc[g, b] = acc[g, b] * shrink + fresh
        run_max[g, b] = new_max

    def partial(g, b, q, place, block, causal):
        start = unit(block)[0] * BLK
        k = own[fixed + g, 0]
        s = lax.dot_general(k, q, (((1,), (1,)), ((), ())), preferred_element_type=jnp.float32)
        key = lax.broadcasted_iota(jnp.int32, (both, ratio * BLK), 0) + first * BLK
        visible = key >= start
        if causal:
            lane = lax.broadcasted_iota(jnp.int32, (both, ratio * BLK), 1)
            visible = visible & (key <= (lane & (BLK - 1)) + block * BLK)
        s = jnp.where(visible, s * SCALE, HIDDEN)
        top = jnp.maximum(jnp.max(s, axis=0, keepdims=True), FLOOR)
        p = jnp.exp2(s - top)
        total = jnp.sum(p, axis=0, keepdims=True)
        summed = jnp.dot(turned[g], p.astype(jnp.bfloat16), preferred_element_type=jnp.float32)
        for j in range(ratio):
            lanes = slice(j * BLK, (j + 1) * BLK)
            part[g % 2, place, b, j] = summed[:, lanes]
            part_stat[g % 2, place, b, pl.ds(j, 1), :] = top[:, lanes]
            part_stat[g % 2, place, b, pl.ds(ratio + j, 1), :] = total[:, lanes]

    def out_copy(head):
        return pltpu.make_async_copy(
            result.at[head, mine], o_hbm.at[:, columns(core * heads_here + head)], out_sem.at[head]
        )

    def back_copy(head, side):
        return pltpu.make_async_remote_copy(
            src_ref=result.at[head, theirs],
            dst_ref=o_hbm.at[:, columns(side * heads_here + head)],
            send_sem=back_send.at[head], recv_sem=back_recv.at[head],
            device_id={"seq": partner}, device_id_type=MESH,
        )

    def finish(g):
        for b in range(blocks):
            value = (acc[g, b] / run_sum[g, b]).astype(jnp.bfloat16).reshape(ratio, BLK, DH)
            result[pl.ds(g * ratio, ratio), pl.ds(b * BLK, BLK), :] = value

    def send_back(g):
        for j in range(ratio):
            back_copy(g * ratio + j, core).start()
            out_copy(g * ratio + j).start()

    def free_slot(phase, slot, b):
        @pl.when(phase >= 2)
        def _():
            hop(sent.at[0, slot, b], phase, slot, b).wait_send()

        @pl.when(phase >= 3)
        def _():
            stat_hop(phase, slot, b).wait_send()

    def chosen(block):
        return jnp.full((BLK, DH), block, jnp.int32) >= keys_from

    def step(index, carry):
        phase = index // (span * blocks)
        slot = (index // blocks) % span
        b = index % blocks
        block_in = first - (1 + slot) * blocks + b

        hop(got.at[phase, slot, b], phase, slot, b).wait_recv()

        @pl.when(phase == 0)
        def _():
            @pl.when(slot < span - 1)
            def _():
                sent[0, slot + 1, b] = got[0, slot, b]

        @pl.when(phase > 0)
        def _():
            stat_hop(phase, slot, b).wait_recv()
            turn = (phase - 1) % 2
            place = jnp.where(slot == span - 1, span, span - 2 - slot)
            usable = jnp.full((1, BLK), block_in + span * blocks, jnp.int32) < sums_to
            sums = []
            for j in range(ratio):
                came = jnp.where(usable, got_stat[phase, slot, b, pl.ds(j, 1), :], HIDDEN)
                top = part_stat[turn, place, b, pl.ds(j, 1), :]
                total = part_stat[turn, place, b, pl.ds(ratio + j, 1), :]
                peak = jnp.maximum(came, top)
                keep = jnp.exp2(came - peak)
                add = jnp.exp2(top - peak)
                weight = jnp.maximum(keep + add * total, 1.0)
                share = 1.0 / weight
                mixed = got[phase, slot, b, j].astype(jnp.float32) * (keep * share) + part[
                    turn, place, b, j
                ] * (add * share)
                sums.append((mixed, peak + jnp.log2(weight)))

            @pl.when(slot < span - 1)
            def _():
                free_slot(phase, slot + 1, b)
                pick = chosen(block_in)
                for j in range(ratio):
                    sent[phase % 2, slot + 1, b, j] = jnp.where(
                        pick, got[phase, slot, b, j], sums[j][0].astype(jnp.bfloat16)
                    )
                    sent_stat[phase % 2, slot + 1, b, pl.ds(j, 1), :] = sums[j][1]

            @pl.when(slot == span - 1)
            def _():
                for j in range(ratio):
                    head = (fixed + phase - 1) * ratio + j
                    result[head, block_rows(b), :] = sums[j][0].T.astype(jnp.bfloat16)

        @pl.when(phase < fixed)
        def _():
            q_hop(q_got.at[phase, slot, b], phase, slot, b).wait_recv()

            @pl.when(slot < span - 1)
            def _():
                q_hop(q_got.at[phase, slot, b], phase, slot + 1, b).start()

        @pl.when(slot < span - 1)
        def _():
            hop(sent.at[phase % 2, slot + 1, b], phase, slot + 1, b).start()

            @pl.when(phase > 0)
            def _():
                stat_hop(phase, slot + 1, b).start()

        @pl.when(phase < fixed)
        def _():
            partial(
                phase, b, q_got[phase, slot, b].reshape(ratio * BLK, DH), slot,
                first + (1 + slot) * blocks + b, False,
            )

            @pl.when(slot == 0)
            def _():
                q = q_all[pl.ds((fixed + phase) * ratio, ratio), block_rows(b), :]
                partial(phase, b, q.reshape(ratio * BLK, DH), span, first + b, True)
                flash(phase, b, own[phase, 0], own[phase, 1], first * BLK, True)

            @pl.when(slot == span - 1)
            def _():
                after = phase + 1
                free_slot(after, 0, b)
                pick = chosen(first + b)
                head = jnp.minimum(after, fixed - 1)
                for j in range(ratio):
                    top = part_stat[phase % 2, span - 1, b, pl.ds(j, 1), :]
                    weight = jnp.maximum(part_stat[phase % 2, span - 1, b, pl.ds(ratio + j, 1), :], 1.0)
                    summed = part[phase % 2, span - 1, b, j] * (1.0 / weight)
                    sent[after % 2, 0, b, j] = jnp.where(
                        pick, own[head, j, block_rows(b), :], summed.astype(jnp.bfloat16)
                    )
                    sent_stat[after % 2, 0, b, pl.ds(j, 1), :] = top + jnp.log2(weight)

                @pl.when(after < fixed)
                def _():
                    q_hop(own_q(after, b), after, 0, b).start()

                hop(sent.at[after % 2, 0, b], after, 0, b).start()
                stat_hop(after, 0, b).start()

        last = index // blocks - 1

        @pl.when((last >= 0) & (last < fixed * span))
        def _():
            g = last // span
            place = last % span
            k = got[g, place, :, 0].reshape(both, DH)
            v = got[g, place, :, 1].reshape(both, DH)
            flash(g, b, k, v, (chip - 1 - place) * both, False)

        @pl.when((phase == fixed) & (slot >= 1) & (slot <= fixed) & (b == 0))
        def _():
            finish(slot - 1)
            send_back(slot - 1)

        @pl.when((phase > 0) & (slot == span - 1) & (b == blocks - 1))
        def _():
            send_back(fixed + phase - 1)

        return carry

    lax.fori_loop(0, (fixed + 1) * span * blocks, step, 0)

    def drain(g, carry):
        for entry in kv_pieces(g, 1 - core, mine) + q_pieces(g, 1 - core, mine):
            pair_copy(entry).wait_send()
        for j in range(ratio):
            head = g * ratio + j
            out_copy(head).wait()
            back_copy(head, core).wait_send()
            back_copy(head, 1 - core).wait_recv()
        return carry

    lax.fori_loop(0, keys_here, drain, 0)

    def drain_ring(index, carry):
        slot = index // blocks
        b = index % blocks
        for phase in range(fixed):
            q_hop(q_got.at[phase, slot, b], phase, slot, b).wait_send()
        for phase in range(max(fixed - 1, 0), fixed + 1):
            hop(sent.at[0, slot, b], phase, slot, b).wait_send()
        for phase in range(max(fixed - 1, 1), fixed + 1):
            stat_hop(phase, slot, b).wait_send()
        return carry

    lax.fori_loop(0, span * blocks, drain_ring, 0)


def on_device(queries, keys, values, doc_blocks):
    rows = queries.shape[0]
    both = 2 * rows
    chips = lax.axis_size("seq") // 2
    heads_here = queries.shape[1] // DH // 2
    keys_here = keys.shape[1] // DH // 2
    ratio = heads_here // keys_here
    fixed = keys_here // 2
    blocks = both // BLK
    span = MAX_UNITS // blocks
    state = (fixed, blocks, ratio * BLK, DH)
    slots = (span, blocks)
    pieces = 2 * keys_here + heads_here
    dma = pltpu.SemaphoreType.DMA
    anywhere = pl.BlockSpec(memory_space=pl.ANY)
    return pl.pallas_call(
        functools.partial(kernel, chips, span),
        out_shape=jax.ShapeDtypeStruct(queries.shape, queries.dtype),
        in_specs=[pl.BlockSpec(memory_space=pltpu.SMEM)] + [anywhere] * 3,
        out_specs=anywhere,
        scratch_shapes=[
            pltpu.VMEM((heads_here, both, DH), jnp.bfloat16),
            pltpu.VMEM((keys_here, 2, both, DH), jnp.bfloat16),
            pltpu.VMEM((fixed, DH, both), jnp.bfloat16),
            pltpu.VMEM((fixed + 1,) + slots + (2, BLK, DH), jnp.bfloat16),
            pltpu.VMEM((2,) + slots + (2, BLK, DH), jnp.bfloat16),
            pltpu.VMEM((fixed + 1,) + slots + (ratio, BLK), jnp.float32),
            pltpu.VMEM((2,) + slots + (ratio, BLK), jnp.float32),
            pltpu.VMEM((fixed,) + slots + (ratio, BLK, DH), jnp.bfloat16),
            pltpu.VMEM(state, jnp.float32),
            pltpu.VMEM(state, jnp.float32),
            pltpu.VMEM(state, jnp.float32),
            pltpu.VMEM((2, span + 1, blocks, ratio, DH, BLK), jnp.float32),
            pltpu.VMEM((2, span + 1, blocks, 2 * ratio, BLK), jnp.float32),
            pltpu.VMEM((heads_here, both, DH), jnp.bfloat16),
            dma((pieces,)),
            dma((pieces,)),
            dma((pieces,)),
            dma((2,) + slots),
            dma((fixed + 1,) + slots),
            dma((2,) + slots),
            dma((fixed + 1,) + slots),
            dma((fixed,) + slots),
            dma((fixed,) + slots),
            dma((heads_here,)),
            dma((heads_here,)),
            dma((heads_here,)),
        ],
        compiler_params=pltpu.CompilerParams(
            collective_id=0, has_side_effects=True, vmem_limit_bytes=62 * 1024 * 1024
        ),
        name="two_way_attention",
    )(doc_blocks, queries, keys, values)


def solution(mesh):
    token = P(("groups", "seq"), None)
    return jax.shard_map(
        on_device, mesh=mesh, in_specs=(token, token, token, P("groups")),
        out_specs=token, check_vma=False,
    )
```

time: 385 us -> 273 us (0.71)
  Pallas kernels: 381 us -> 270 us
    pallas_call x1, Pallas kernels: 381 us -> 270 us  [on_device(): pl.pallas_call(functools.partial(kernel, chips, span), out_shape=jax.Shap...]
where the time goes in v1:
time: 273 us
  Pallas kernels  270 us (99%)
  local copies, waits for them, and re-layouts  3.13 us (1%)
    pallas_call x1, Pallas kernels, on_device(): pl.pallas_call(functools.partial(kernel, chips, span), out_shape=jax.Shap...  270 us

profile of v1, /device:TPU:37, one launch (start us, length us, event | category | flops | bytes accessed | tf_op | source)
XLA Modules:
  0.0 273.0 jit_solution(9802126628049665882)
XLA Ops:
  0.0 269.8 %two_way_attention.1 = bf16[256,4096]{1,0:T(8,128)(2,1)} custom-call(s32[8]{0:T(128)} %docs_ref.1, bf16[256,4096]{1,0:T(8,128)(2,1)} %q_hbm.1, bf16[256,2048]{1,0:T(8,128)(2,1)} %k_hbm.1, bf16[256,2048]{1,0:T(8,128)(2,1)} %v_hbm.1), custom_call_target="tpu_custom_call" | custom-call | tf_op jit(solution)/shard_map/two_way_attention/pallas_call | solution.py:424
  269.9 3.1 %copy.6 = bf16[256,4096]{1,0:T(8,128)(2,1)} copy(bf16[256,4096]{1,0:T(8,128)(2,1)} %two_way_attention.1) | data formatting | bytes 4194304

commit v2 on v1

--- a/solution.py
+++ b/solution.py
@@ -27,22 +27,37 @@
 ):
     rows = q_hbm.shape[0]
     both = 2 * rows
-    keys_here = own.shape[0]
-    heads_here = q_all.shape[0]
-    ratio = heads_here // keys_here
+    key_slots = own.shape[0]
+    ratio = q_all.shape[0] // key_slots
     blocks = both // BLK
-    fixed = keys_here // 2
+    half = k_hbm.shape[1] // DH // 2
     me = lax.axis_index("seq")
     core = lax.rem(me, 2)
     chip = lax.div(me, 2)
     partner = me + 1 - 2 * core
     right = lax.rem(chip + 1, chips) * 2 + core
     left = lax.rem(chip + chips - 1, chips) * 2 + core
+    has_left = chip > 0
+    has_right = chip < chips - 1
+
+    moved = half // 2 - 1 + core
+    fixed = moved + 1
+    keys_here = fixed + moved
+    key_base = core * (half - 1)
+    moved_there = half // 2 - core
+    fixed_there = moved_there + 1
+    keys_there = fixed_there + moved_there
+    base_there = (1 - core) * (half - 1)
 
     barrier = pltpu.get_barrier_semaphore()
-    for source in (left, right, partner):
-        pl.semaphore_signal(barrier, inc=1, device_id={"seq": source}, device_id_type=MESH)
-    pl.semaphore_wait(barrier, 3)
+
+    def greet(device):
+        pl.semaphore_signal(barrier, inc=1, device_id={"seq": device}, device_id_type=MESH)
+
+    greet(partner)
+    pl.when(has_left)(lambda: greet(left))
+    pl.when(has_right)(lambda: greet(right))
+    pl.semaphore_wait(barrier, 1 + jnp.minimum(chip, 1) + jnp.minimum(chips - 1 - chip, 1))
 
     mine = pl.ds(pl.multiple_of(core * rows, rows), rows)
     theirs = pl.ds(pl.multiple_of((1 - core) * rows, rows), rows)
@@ -53,22 +68,22 @@
     def block_rows(b):
         return pl.ds(pl.multiple_of(b * BLK, BLK), BLK)
 
-    def kv_pieces(index, side, place):
-        first = side * keys_here + index
+    def kv_pieces(index, base, place):
+        from_head = columns(base + index)
         return [
-            (k_hbm.at[:, columns(first)], own.at[index, 0, place], index),
-            (v_hbm.at[:, columns(first)], own.at[index, 1, place], keys_here + index),
+            (k_hbm.at[:, from_head], own.at[index, 0, place], index),
+            (v_hbm.at[:, from_head], own.at[index, 1, place], key_slots + index),
         ]
 
-    def q_pieces(index, side, place):
+    def q_pieces(index, base, place):
         listed = []
         for j in range(ratio):
             head = index * ratio + j
             listed.append(
                 (
-                    q_hbm.at[:, columns(side * heads_here + head)],
+                    q_hbm.at[:, columns(base * ratio + head)],
                     q_all.at[head, place],
-                    2 * keys_here + head,
+                    2 * key_slots + head,
                 )
             )
         return listed
@@ -83,16 +98,18 @@
             device_id={"seq": partner}, device_id_type=MESH,
         )
 
-    def load(kind, index):
-        for entry in kind(index, 1 - core, mine):
+    def give(kind, index):
+        for entry in kind(index, base_there, mine):
             pair_copy(entry).start()
-        for entry in kind(index, core, mine):
+
+    def take(kind, index):
+        for entry in kind(index, key_base, mine):
             local_copy(entry).start()
 
     def arrive(kind, index):
-        for entry in kind(index, core, mine):
+        for entry in kind(index, key_base, mine):
             local_copy(entry).wait()
-        for entry in kind(index, 1 - core, theirs):
+        for entry in kind(index, key_base, theirs):
             pair_copy(entry).wait_recv()
 
     def hop(source, phase, slot, b):
@@ -119,42 +136,52 @@
     def own_q(phase, b):
         return q_all.at[pl.ds((fixed + phase) * ratio, ratio), block_rows(b)]
 
-    load(kv_pieces, 0)
-    load(q_pieces, fixed)
-
-    def start_rest(g, carry):
-        load(kv_pieces, fixed + g)
-
-        @pl.when(g > 0)
-        def _():
-            load(q_pieces, fixed + g)
-            load(kv_pieces, g)
-
-        load(q_pieces, g)
-        return carry
-
-    lax.fori_loop(0, fixed, start_rest, 0)
+    give(kv_pieces, 0)
+    take(kv_pieces, 0)
+    pl.when(moved_there > 0)(lambda: give(q_pieces, fixed_there))
+    pl.when(moved > 0)(lambda: take(q_pieces, fixed))
+
+    def give_rest(g, carry):
+        pl.when(g > 0)(lambda: give(kv_pieces, g))
+        pl.when(g != fixed_there)(lambda: give(q_pieces, g))
+        return carry
+
+    def take_rest(g, carry):
+        pl.when(g > 0)(lambda: take(kv_pieces, g))
+        pl.when(g != fixed)(lambda: take(q_pieces, g))
+        return carry
+
+    lax.fori_loop(0, keys_there, give_rest, 0)
+    lax.fori_loop(0, keys_here, take_rest, 0)
 
     arrive(kv_pieces, 0)
-    for b in range(blocks):
-        hop(own.at[0, :, block_rows(b)], 0, 0, b).start()
-    arrive(q_pieces, fixed)
-    for b in range(blocks):
-        q_hop(own_q(0, b), 0, 0, b).start()
+
+    @pl.when(has_right)
+    def _():
+        for b in range(blocks):
+            hop(own.at[0, :, block_rows(b)], 0, 0, b).start()
+
+    @pl.when(moved > 0)
+    def _():
+        arrive(q_pieces, fixed)
+
+        @pl.when(has_left)
+        def _():
+            for b in range(blocks):
+                q_hop(own_q(0, b), 0, 0, b).start()
 
     def wait_rest(g, carry):
-        arrive(kv_pieces, fixed + g)
-
-        @pl.when(g > 0)
-        def _():
-            arrive(q_pieces, fixed + g)
-            arrive(kv_pieces, g)
-
-        arrive(q_pieces, g)
+        pl.when(g > 0)(lambda: arrive(kv_pieces, g))
+        pl.when(g != fixed)(lambda: arrive(q_pieces, g))
+        return carry
+
+    lax.fori_loop(0, keys_here, wait_rest, 0)
+
+    def turn_values(g, carry):
         turned[g] = own[fixed + g, 1].astype(jnp.float32).T.astype(jnp.bfloat16)
         return carry
 
-    lax.fori_loop(0, fixed, wait_rest, 0)
+    lax.fori_loop(0, moved, turn_values, 0)
 
     def unit(index):
         total = jnp.int32(0)
@@ -222,13 +249,13 @@
 
     def out_copy(head):
         return pltpu.make_async_copy(
-            result.at[head, mine], o_hbm.at[:, columns(core * heads_here + head)], out_sem.at[head]
+            result.at[head, mine], o_hbm.at[:, columns(key_base * ratio + head)], out_sem.at[head]
         )
 
-    def back_copy(head, side):
+    def back_copy(head, base):
         return pltpu.make_async_remote_copy(
             src_ref=result.at[head, theirs],
-            dst_ref=o_hbm.at[:, columns(side * heads_here + head)],
+            dst_ref=o_hbm.at[:, columns(base * ratio + head)],
             send_sem=back_send.at[head], recv_sem=back_recv.at[head],
             device_id={"seq": partner}, device_id_type=MESH,
         )
@@ -240,7 +267,7 @@
 
     def send_back(g):
         for j in range(ratio):
-            back_copy(g * ratio + j, core).start()
+            back_copy(g * ratio + j, key_base).start()
             out_copy(g * ratio + j).start()
 
     def free_slot(phase, slot, b):
@@ -254,6 +281,16 @@
 
     def chosen(block):
         return jnp.full((BLK, DH), block, jnp.int32) >= keys_from
+
+    def forward_flash(last, b):
+        g = last // span
+        place = last % span
+
+        @pl.when((last >= 0) & (chip - 1 - place >= 0))
+        def _():
+            k = got[g, place, :, 0].reshape(both, DH)
+            v = got[g, place, :, 1].reshape(both, DH)
+            flash(g, b, k, v, (chip - 1 - place) * both, False)
 
     def step(index, carry):
         phase = index // (span * blocks)
@@ -261,20 +298,28 @@
         b = index % blocks
         block_in = first - (1 + slot) * blocks + b
 
-        hop(got.at[phase, slot, b], phase, slot, b).wait_recv()
-
-        @pl.when(phase == 0)
-        def _():
-            @pl.when(slot < span - 1)
+        @pl.when(has_left)
+        def _():
+            hop(got.at[phase, slot, b], phase, slot, b).wait_recv()
+            pl.when(phase > 0)(lambda: stat_hop(phase, slot, b).wait_recv())
+
+        @pl.when((phase == 0) & (slot < span - 1))
+        def _():
+            @pl.when(has_left)
             def _():
                 sent[0, slot + 1, b] = got[0, slot, b]
 
+            @pl.when(chip == 0)
+            def _():
+                sent[0, slot + 1, b] = jnp.zeros((2, BLK, DH), jnp.bfloat16)
+
         @pl.when(phase > 0)
         def _():
-            stat_hop(phase, slot, b).wait_recv()
             turn = (phase - 1) % 2
             place = jnp.where(slot == span - 1, span, span - 2 - slot)
-            usable = jnp.full((1, BLK), block_in + span * blocks, jnp.int32) < sums_to
+            home = block_in + span * blocks
+            usable = jnp.full((1, BLK), home, jnp.int32) < sums_to
+            usable_block = jnp.full((DH, BLK), home, jnp.int32) < sums_to
             sums = []
             for j in range(ratio):
                 came = jnp.where(usable, got_stat[phase, slot, b, pl.ds(j, 1), :], HIDDEN)
@@ -285,12 +330,11 @@
                 add = jnp.exp2(top - peak)
                 weight = jnp.maximum(keep + add * total, 1.0)
                 share = 1.0 / weight
-                mixed = got[phase, slot, b, j].astype(jnp.float32) * (keep * share) + part[
-                    turn, place, b, j
-                ] * (add * share)
+                arrived = jnp.where(usable_block, got[phase, slot, b, j].astype(jnp.float32), 0.0)
+                mixed = arrived * (keep * share) + part[turn, place, b, j] * (add * share)
                 sums.append((mixed, peak + jnp.log2(weight)))
 
-            @pl.when(slot < span - 1)
+            @pl.when((slot < span - 1) & has_right)
             def _():
                 free_slot(phase, slot + 1, b)
                 pick = chosen(block_in)
@@ -306,15 +350,15 @@
                     head = (fixed + phase - 1) * ratio + j
                     result[head, block_rows(b), :] = sums[j][0].T.astype(jnp.bfloat16)
 
-        @pl.when(phase < fixed)
+        @pl.when((phase < moved) & (chip + 1 + slot < chips))
         def _():
             q_hop(q_got.at[phase, slot, b], phase, slot, b).wait_recv()
 
-            @pl.when(slot < span - 1)
+            @pl.when((slot < span - 1) & has_left)
             def _():
                 q_hop(q_got.at[phase, slot, b], phase, slot + 1, b).start()
 
-        @pl.when(slot < span - 1)
+        @pl.when((slot < span - 1) & has_right)
         def _():
             hop(sent.at[phase % 2, slot + 1, b], phase, slot + 1, b).start()
 
@@ -322,7 +366,7 @@
             def _():
                 stat_hop(phase, slot + 1, b).start()
 
-        @pl.when(phase < fixed)
+        @pl.when(phase < moved)
         def _():
             partial(
                 phase, b, q_got[phase, slot, b].reshape(ratio * BLK, DH), slot,
@@ -333,44 +377,36 @@
             def _():
                 q = q_all[pl.ds((fixed + phase) * ratio, ratio), block_rows(b), :]
                 partial(phase, b, q.reshape(ratio * BLK, DH), span, first + b, True)
-                flash(phase, b, own[phase, 0], own[phase, 1], first * BLK, True)
-
-            @pl.when(slot == span - 1)
+
+            @pl.when((slot == span - 1) & has_right)
             def _():
                 after = phase + 1
                 free_slot(after, 0, b)
                 pick = chosen(first + b)
-                head = jnp.minimum(after, fixed - 1)
                 for j in range(ratio):
                     top = part_stat[phase % 2, span - 1, b, pl.ds(j, 1), :]
                     weight = jnp.maximum(part_stat[phase % 2, span - 1, b, pl.ds(ratio + j, 1), :], 1.0)
                     summed = part[phase % 2, span - 1, b, j] * (1.0 / weight)
                     sent[after % 2, 0, b, j] = jnp.where(
-                        pick, own[head, j, block_rows(b), :], summed.astype(jnp.bfloat16)
+                        pick, own[after, j, block_rows(b), :], summed.astype(jnp.bfloat16)
                     )
                     sent_stat[after % 2, 0, b, pl.ds(j, 1), :] = top + jnp.log2(weight)
 
-                @pl.when(after < fixed)
-                def _():
-                    q_hop(own_q(after, b), after, 0, b).start()
-
                 hop(sent.at[after % 2, 0, b], after, 0, b).start()
                 stat_hop(after, 0, b).start()
 
-        last = index // blocks - 1
-
-        @pl.when((last >= 0) & (last < fixed * span))
-        def _():
-            g = last // span
-            place = last % span
-            k = got[g, place, :, 0].reshape(both, DH)
-            v = got[g, place, :, 1].reshape(both, DH)
-            flash(g, b, k, v, (chip - 1 - place) * both, False)
-
-        @pl.when((phase == fixed) & (slot >= 1) & (slot <= fixed) & (b == 0))
-        def _():
-            finish(slot - 1)
-            send_back(slot - 1)
+            @pl.when((slot == span - 1) & has_left & (phase + 1 < moved))
+            def _():
+                q_hop(own_q(phase + 1, b), phase + 1, 0, b).start()
+
+        forward_flash(index // blocks - 1, b)
+
+        @pl.when(slot == 0)
+        def _():
+            flash(phase, b, own[phase, 0], own[phase, 1], first * BLK, True)
+
+        pl.when((phase > 0) & (slot == 1) & (b == 0))(lambda: finish(phase - 1))
+        pl.when((phase > 0) & (slot == 1) & (b == 1))(lambda: send_back(phase - 1))
 
         @pl.when((phase > 0) & (slot == span - 1) & (b == blocks - 1))
         def _():
@@ -378,47 +414,77 @@
 
         return carry
 
-    lax.fori_loop(0, (fixed + 1) * span * blocks, step, 0)
-
-    def drain(g, carry):
-        for entry in kv_pieces(g, 1 - core, mine) + q_pieces(g, 1 - core, mine):
+    lax.fori_loop(0, fixed * span * blocks, step, 0)
+
+    def final_flash(b, carry):
+        forward_flash(fixed * span - 1, b)
+        return carry
+
+    lax.fori_loop(0, blocks, final_flash, 0)
+    finish(fixed - 1)
+    send_back(fixed - 1)
+
+    def drain_given(g, carry):
+        for entry in kv_pieces(g, base_there, mine) + q_pieces(g, base_there, mine):
             pair_copy(entry).wait_send()
         for j in range(ratio):
-            head = g * ratio + j
-            out_copy(head).wait()
-            back_copy(head, core).wait_send()
-            back_copy(head, 1 - core).wait_recv()
-        return carry
-
-    lax.fori_loop(0, keys_here, drain, 0)
+            back_copy(g * ratio + j, base_there).wait_recv()
+        return carry
+
+    lax.fori_loop(0, keys_there, drain_given, 0)
 
     def drain_ring(index, carry):
         slot = index // blocks
         b = index % blocks
-        for phase in range(fixed):
+
+        def q_sent(phase, inner):
             q_hop(q_got.at[phase, slot, b], phase, slot, b).wait_send()
-        for phase in range(max(fixed - 1, 0), fixed + 1):
+            return inner
+
+        def block_sent(phase, inner):
             hop(sent.at[0, slot, b], phase, slot, b).wait_send()
-        for phase in range(max(fixed - 1, 1), fixed + 1):
+            return inner
+
+        def stat_sent(phase, inner):
             stat_hop(phase, slot, b).wait_send()
+            return inner
+
+        @pl.when(has_left & (chip + slot < chips))
+        def _():
+            lax.fori_loop(0, moved, q_sent, 0)
+
+        @pl.when(has_right)
+        def _():
+            lax.fori_loop(jnp.maximum(fixed - 2, 0), fixed, block_sent, 0)
+            lax.fori_loop(jnp.maximum(fixed - 2, 1), fixed, stat_sent, 0)
+
         return carry
 
     lax.fori_loop(0, span * blocks, drain_ring, 0)
+
+    def drain_out(head, carry):
+        out_copy(head).wait()
+        back_copy(head, key_base).wait_send()
+        return carry
+
+    lax.fori_loop(0, keys_here * ratio, drain_out, 0)
 
 
 def on_device(queries, keys, values, doc_blocks):
     rows = queries.shape[0]
     both = 2 * rows
     chips = lax.axis_size("seq") // 2
-    heads_here = queries.shape[1] // DH // 2
-    keys_here = keys.shape[1] // DH // 2
-    ratio = heads_here // keys_here
-    fixed = keys_here // 2
+    half = keys.shape[1] // DH // 2
+    ratio = queries.shape[1] // keys.shape[1]
+    key_slots = half + 1
+    head_slots = key_slots * ratio
+    moved = half // 2
+    fixed = moved + 1
     blocks = both // BLK
     span = MAX_UNITS // blocks
     state = (fixed, blocks, ratio * BLK, DH)
     slots = (span, blocks)
-    pieces = 2 * keys_here + heads_here
+    pieces = 2 * key_slots + head_slots
     dma = pltpu.SemaphoreType.DMA
     anywhere = pl.BlockSpec(memory_space=pl.ANY)
     return pl.pallas_call(
@@ -427,32 +493,32 @@
         in_specs=[pl.BlockSpec(memory_space=pltpu.SMEM)] + [anywhere] * 3,
         out_specs=anywhere,
         scratch_shapes=[
-            pltpu.VMEM((heads_here, both, DH), jnp.bfloat16),
-            pltpu.VMEM((keys_here, 2, both, DH), jnp.bfloat16),
-            pltpu.VMEM((fixed, DH, both), jnp.bfloat16),
-            pltpu.VMEM((fixed + 1,) + slots + (2, BLK, DH), jnp.bfloat16),
+            pltpu.VMEM((head_slots, both, DH), jnp.bfloat16),
+            pltpu.VMEM((key_slots, 2, both, DH), jnp.bfloat16),
+            pltpu.VMEM((moved, DH, both), jnp.bfloat16),
+            pltpu.VMEM((fixed,) + slots + (2, BLK, DH), jnp.bfloat16),
             pltpu.VMEM((2,) + slots + (2, BLK, DH), jnp.bfloat16),
-            pltpu.VMEM((fixed + 1,) + slots + (ratio, BLK), jnp.float32),
+            pltpu.VMEM((fixed,) + slots + (ratio, BLK), jnp.float32),
             pltpu.VMEM((2,) + slots + (ratio, BLK), jnp.float32),
-            pltpu.VMEM((fixed,) + slots + (ratio, BLK, DH), jnp.bfloat16),
+            pltpu.VMEM((moved,) + slots + (ratio, BLK, DH), jnp.bfloat16),
             pltpu.VMEM(state, jnp.float32),
             pltpu.VMEM(state, jnp.float32),
             pltpu.VMEM(state, jnp.float32),
             pltpu.VMEM((2, span + 1, blocks, ratio, DH, BLK), jnp.float32),
             pltpu.VMEM((2, span + 1, blocks, 2 * ratio, BLK), jnp.float32),
-            pltpu.VMEM((heads_here, both, DH), jnp.bfloat16),
+            pltpu.VMEM((head_slots, both, DH), jnp.bfloat16),
             dma((pieces,)),
             dma((pieces,)),
             dma((pieces,)),
             dma((2,) + slots),
-            dma((fixed + 1,) + slots),
+            dma((fixed,) + slots),
             dma((2,) + slots),
-            dma((fixed + 1,) + slots),
             dma((fixed,) + slots),
-            dma((fixed,) + slots),
-            dma((heads_here,)),
-            dma((heads_here,)),
-            dma((heads_here,)),
+            dma((moved,) + slots),
+            dma((moved,) + slots),
+            dma((head_slots,)),
+            dma((head_slots,)),
+            dma((head_slots,)),
         ],
         compiler_params=pltpu.CompilerParams(
             collective_id=0, has_side_effects=True, vmem_limit_bytes=62 * 1024 * 1024

time: 273 us -> 244 us (0.89)
  the two profiles are of different devices: /device:TPU:37 before, /device:TPU:748 now
where the time goes in v2:
time: 244 us
  Pallas kernels  241 us (99%)
  local copies, waits for them, and re-layouts  3.13 us (1%)
    pallas_call x1, Pallas kernels, on_device(): pl.pallas_call(functools.partial(kernel, chips, span), out_shape=jax.Shap...  241 us

profile of v2, /device:TPU:748, one launch (start us, length us, event | category | flops | bytes accessed | tf_op | source)
XLA Modules:
  0.0 243.8 jit_solution(11976244273642936400)
XLA Ops:
  0.0 240.7 %two_way_attention.1 = bf16[256,4096]{1,0:T(8,128)(2,1)} custom-call(s32[8]{0:T(128)} %docs_ref.1, bf16[256,4096]{1,0:T(8,128)(2,1)} %q_hbm.1, bf16[256,2048]{1,0:T(8,128)(2,1)} %k_hbm.1, bf16[256,2048]{1,0:T(8,128)(2,1)} %v_hbm.1), custom_call_target="tpu_custom_call" | custom-call | tf_op jit(solution)/shard_map/two_way_attention/pallas_call | solution.py:490
  240.7 3.1 %copy.6 = bf16[256,4096]{1,0:T(8,128)(2,1)} copy(bf16[256,4096]{1,0:T(8,128)(2,1)} %two_way_attention.1) | data formatting | bytes 4194304

commit v3 on v2

--- a/solution.py
+++ b/solution.py
@@ -270,17 +270,13 @@
             back_copy(g * ratio + j, key_base).start()
             out_copy(g * ratio + j).start()
 
-    def free_slot(phase, slot, b):
-        @pl.when(phase >= 2)
-        def _():
-            hop(sent.at[0, slot, b], phase, slot, b).wait_send()
-
-        @pl.when(phase >= 3)
-        def _():
-            stat_hop(phase, slot, b).wait_send()
-
     def chosen(block):
         return jnp.full((BLK, DH), block, jnp.int32) >= keys_from
+
+    def drain_given(g, carry):
+        for entry in kv_pieces(g, base_there, mine) + q_pieces(g, base_there, mine):
+            pair_copy(entry).wait_send()
+        return carry
 
     def forward_flash(last, b):
         g = last // span
@@ -336,7 +332,6 @@
 
             @pl.when((slot < span - 1) & has_right)
             def _():
-                free_slot(phase, slot + 1, b)
                 pick = chosen(block_in)
                 for j in range(ratio):
                     sent[phase % 2, slot + 1, b, j] = jnp.where(
@@ -373,7 +368,7 @@
                 first + (1 + slot) * blocks + b, False,
             )
 
-            @pl.when(slot == 0)
+            @pl.when(slot == 2)
             def _():
                 q = q_all[pl.ds((fixed + phase) * ratio, ratio), block_rows(b), :]
                 partial(phase, b, q.reshape(ratio * BLK, DH), span, first + b, True)
@@ -381,7 +376,6 @@
             @pl.when((slot == span - 1) & has_right)
             def _():
                 after = phase + 1
-                free_slot(after, 0, b)
                 pick = chosen(first + b)
                 for j in range(ratio):
                     top = part_stat[phase % 2, span - 1, b, pl.ds(j, 1), :]
@@ -401,12 +395,26 @@
 
         forward_flash(index // blocks - 1, b)
 
-        @pl.when(slot == 0)
-        def _():
-            flash(phase, b, own[phase, 0], own[phase, 1], first * BLK, True)
+        @pl.when((index < blocks) | ((slot == 4) & (phase < moved)))
+        def _():
+            g = jnp.where(slot == 4, phase + 1, 0)
+            flash(g, b, own[g, 0], own[g, 1], first * BLK, True)
 
         pl.when((phase > 0) & (slot == 1) & (b == 0))(lambda: finish(phase - 1))
         pl.when((phase > 0) & (slot == 1) & (b == 1))(lambda: send_back(phase - 1))
+
+        @pl.when((phase > 0) & has_right)
+        def _():
+            hop(sent.at[0, slot, b], phase - 1, slot, b).wait_send()
+            pl.when(phase > 1)(lambda: stat_hop(phase - 1, slot, b).wait_send())
+
+        @pl.when((phase > 0) & has_left & (chip + slot < chips))
+        def _():
+            q_hop(q_got.at[0, slot, b], phase - 1, slot, b).wait_send()
+
+        @pl.when(index == 3 * blocks)
+        def _():
+            lax.fori_loop(0, keys_there, drain_given, 0)
 
         @pl.when((phase > 0) & (slot == span - 1) & (b == blocks - 1))
         def _():
@@ -424,43 +432,16 @@
     finish(fixed - 1)
     send_back(fixed - 1)
 
-    def drain_given(g, carry):
-        for entry in kv_pieces(g, base_there, mine) + q_pieces(g, base_there, mine):
-            pair_copy(entry).wait_send()
-        for j in range(ratio):
-            back_copy(g * ratio + j, base_there).wait_recv()
-        return carry
-
-    lax.fori_loop(0, keys_there, drain_given, 0)
-
     def drain_ring(index, carry):
         slot = index // blocks
         b = index % blocks
-
-        def q_sent(phase, inner):
-            q_hop(q_got.at[phase, slot, b], phase, slot, b).wait_send()
-            return inner
-
-        def block_sent(phase, inner):
-            hop(sent.at[0, slot, b], phase, slot, b).wait_send()
-            return inner
-
-        def stat_sent(phase, inner):
-            stat_hop(phase, slot, b).wait_send()
-            return inner
-
-        @pl.when(has_left & (chip + slot < chips))
-        def _():
-            lax.fori_loop(0, moved, q_sent, 0)
-
-        @pl.when(has_right)
-        def _():
-            lax.fori_loop(jnp.maximum(fixed - 2, 0), fixed, block_sent, 0)
-            lax.fori_loop(jnp.maximum(fixed - 2, 1), fixed, stat_sent, 0)
-
-        return carry
-
-    lax.fori_loop(0, span * blocks, drain_ring, 0)
+        hop(sent.at[0, slot, b], fixed - 1, slot, b).wait_send()
+        pl.when(fixed > 1)(lambda: stat_hop(fixed - 1, slot, b).wait_send())
+        return carry
+
+    @pl.when(has_right)
+    def _():
+        lax.fori_loop(0, span * blocks, drain_ring, 0)
 
     def drain_out(head, carry):
         out_copy(head).wait()
@@ -468,6 +449,12 @@
         return carry
 
     lax.fori_loop(0, keys_here * ratio, drain_out, 0)
+
+    def drain_back(head, carry):
+        back_copy(head, base_there).wait_recv()
+        return carry
+
+    lax.fori_loop(0, keys_there * ratio, drain_back, 0)
 
 
 def on_device(queries, keys, values, doc_blocks):

time: 244 us -> 241 us (0.988)
  the two profiles are of different devices: /device:TPU:748 before, /device:TPU:37 now
where the time goes in v3:
time: 241 us; the launch traced here: 239 us
  Pallas kernels  235 us (98%)
  local copies, waits for them, and re-layouts  3.13 us (1%)
    pallas_call x1, Pallas kernels, on_device(): pl.pallas_call(functools.partial(kernel, chips, span), out_shape=jax.Shap...  235 us

profile of v3, /device:TPU:37, one launch (start us, length us, event | category | flops | bytes accessed | tf_op | source)
XLA Modules:
  0.0 238.5 jit_solution(14337344892539728050)
XLA Ops:
  0.0 235.4 %two_way_attention.1 = bf16[256,4096]{1,0:T(8,128)(2,1)} custom-call(s32[8]{0:T(128)} %docs_ref.1, bf16[256,4096]{1,0:T(8,128)(2,1)} %q_hbm.1, bf16[256,2048]{1,0:T(8,128)(2,1)} %k_hbm.1, bf16[256,2048]{1,0:T(8,128)(2,1)} %v_hbm.1), custom_call_target="tpu_custom_call" | custom-call | tf_op jit(solution)/shard_map/two_way_attention/pallas_call | solution.py:477
  235.4 3.1 %copy.6 = bf16[256,4096]{1,0:T(8,128)(2,1)} copy(bf16[256,4096]{1,0:T(8,128)(2,1)} %two_way_attention.1) | data formatting | bytes 4194304
